TPU v7x, 1024 devices: a whole 4x8x16 slice. The times are simulated.
1024 devices in a mesh: dp: 16 (over x, y_lo), mp: 64 (over z, y_hi, core).
Axes of the slice: x: 4, y: 8 (y_hi: 2, y_lo: 4; y = y_hi * 4 + y_lo), z: 16, core: 2. Of those that a mesh axis runs over, the one named last changes fastest.
Arguments:
- tokens: bfloat16 [2048, 6144], P(('dp', 'mp')), may hold values from -6 to 6
- norm_gain: float32 [6144], replicated, may hold values from 0.5 to 1.5
- up_weight: bfloat16 [6144, 16384], P(None, 'mp'), may hold values from -0.078125 to 0.078125
- down_weight: bfloat16 [16384, 6144], P('mp'), may hold values from -0.046875 to 0.046875
- out_grad: bfloat16 [2048, 6144], P(('dp', 'mp')), may hold values from -6 to 6
Outputs:
- input_grad: bfloat16 [2048, 6144], P(('dp', 'mp'))
- up_grad: bfloat16 [6144, 16384], P('dp', 'mp')
- down_grad: bfloat16 [16384, 6144], P('mp', 'dp')
- gain_grad: float32 [6144], replicated
All inputs are finite; a program needn't handle non-finite values.
Results may differ from a plain program's by a relative error of at most 0.018.
Values may be sent and summed in bfloat16 or wider, within the bound.
A program may use at most 64 MiB of HBM per device.

v0:
```python
import functools
import math

import jax
import jax.numpy as jnp
from jax import lax
from jax.sharding import Mesh
from jax.sharding import PartitionSpec as P

MP = ("mp_0", "mp_1", "mp_2")
DP = ("dp_0", "dp_1")
DP_MP = ("dp_0", "dp_1", "mp_0", "mp_1", "mp_2")


def side_by_side(arrays, axis, dim, along):
    ends, at = ([], 0)
    for a in arrays[:-1]:
        at += a.shape[along]
        ends.append(at)
    both = jnp.concatenate(arrays, axis=along)
    return tuple(jnp.split(lax.all_gather(both, axis, axis=dim, tiled=True), ends, axis=along))


def sum_in_order(blocks, axes, turns):
    lengths = [lax.axis_size(a) for a in axes]
    blocks = blocks.reshape(*lengths, *blocks.shape[1:])
    blocks = blocks.transpose(*turns, *range(len(axes), blocks.ndim))
    blocks = blocks.reshape(-1, *blocks.shape[len(axes) :])
    for k in turns:
        blocks = lax.psum_scatter(blocks, axes[k], scatter_dimension=0, tiled=True)
    return blocks[0]


def cut_along(shard, dim, length):
    lengths = shard.shape
    blocks = shard.reshape(*lengths[:dim], length, lengths[dim] // length, *lengths[dim + 1 :])
    return jnp.moveaxis(blocks, dim, 0)


def summed_rows_2(shard, axes, turns, dim):
    length = lax.axis_size(axes)
    return sum_in_order(cut_along(shard, dim, length), axes, turns)


def over_axes(shard, axes):
    return functools.reduce(lax.psum, axes, shard)


def sum_packed(arrays, axis, dims):
    length = lax.axis_size(axis)
    blocks = [cut_along(a, dim, length) for a, dim in zip(arrays, dims)]
    lines = jnp.concatenate([b.reshape(length, -1) for b in blocks], axis=1)
    width = max(16, -(-lines.shape[1] // 1024) * 8)
    lines = jnp.pad(lines, ((0, 0), (0, width * 128 - lines.shape[1]))).reshape(-1, 128)
    flat, at, outs = (lax.psum_scatter(lines, axis, tiled=True).reshape(-1), 0, [])
    for b in blocks:
        part = b[0]
        outs.append(flat[at : at + part.size].reshape(part.shape))
        at += part.size
    return tuple(outs)


def gelu_value(preact):
    return 0.5 * preact * (1.0 + lax.erf(preact * 0.7071067811865476))


def gelu_slope(preact):
    return (
        0.5 * (1.0 + lax.erf(preact * 0.7071067811865476))
        + preact * jnp.exp(-0.5 * preact * preact) * 0.3989422804014327
    )


def contract_rows(left, right):
    return lax.dot_general(
        left, right, (((0,), (0,)), ((), ())), preferred_element_type=jnp.float32
    )


def per_device(tokens, norm_gain, up_weight, down_weight, out_grad):
    values = tokens.astype(jnp.float32)
    centered = values - jnp.mean(values, axis=1, keepdims=True)
    inv_std = lax.rsqrt(jnp.mean(centered * centered, axis=1, keepdims=True) + 1e-06)
    x_hat = centered * inv_std
    normed = (x_hat * norm_gain).astype(jnp.bfloat16)
    normed_all, cotan_all = side_by_side((normed, out_grad), MP, 0, 1)
    preact = jnp.dot(normed_all, up_weight, preferred_element_type=jnp.float32)
    hidden = gelu_value(preact).astype(jnp.bfloat16)
    hid_grad = lax.dot_general(
        cotan_all, down_weight, (((1,), (1,)), ((), ())), preferred_element_type=jnp.float32
    )
    pre_grad = (hid_grad * gelu_slope(preact)).astype(jnp.bfloat16)
    norm_grad = summed_rows_2(
        lax.dot_general(
            pre_grad, up_weight, (((1,), (1,)), ((), ())), preferred_element_type=jnp.float32
        ),
        MP,
        (2, 0, 1),
        0,
    )
    replicas = lax.axis_size(DP)
    group = normed_all.shape[0]
    factor = 1.0 / math.sqrt(group * replicas)
    gain_grad = over_axes(jnp.sum(norm_grad * x_hat, axis=0), DP_MP) * factor
    scaled = norm_gain * norm_grad
    input_grad = (
        scaled
        - jnp.mean(scaled, axis=1, keepdims=True)
        - x_hat * jnp.mean(scaled * x_hat, axis=1, keepdims=True)
    ) * inv_std
    up_part = contract_rows(normed_all, pre_grad)
    down_part = contract_rows(hidden, cotan_all)
    up_total, down_total = tuple(
        (
            part.astype(jnp.float32)
            for part in sum_packed(
                (up_part.astype(jnp.bfloat16), down_part.astype(jnp.bfloat16)), DP, (0, 1)
            )
        )
    )
    up_grad = (up_total * factor).astype(jnp.bfloat16)
    down_grad = (down_total * factor).astype(jnp.bfloat16)
    return (input_grad.astype(jnp.bfloat16), up_grad, down_grad, gain_grad)


def solution(mesh):
    torus = Mesh(mesh.devices.reshape(4, 4, 16, 2, 2), ("dp_0", "dp_1", "mp_0", "mp_1", "mp_2"))
    return jax.shard_map(
        per_device,
        mesh=torus,
        in_specs=(P(DP_MP, None), P(), P(None, MP), P(MP, None), P(DP_MP, None)),
        out_specs=(P(DP_MP, None), P(DP, MP), P(MP, DP), P()),
        check_vma=False,
    )
```

profile of v0, /device:TPU:1, one launch (start us, length us, event | category | flops | bytes accessed | tf_op | source)
XLA Modules:
  0.0 621.6 jit_solution(7507563439356959797)
XLA Ops:
  7.2 0.0 all-gather.3.cloned.1.call-start
  7.2 1.1 convert_reduce_fusion
  8.3 1.0 fusion.19
  9.3 0.9 multiply_convert_fusion.5
  10.1 1.4 maximum_bitcast_fusion
  11.5 0.0 all-gather.3.cloned.1.call-update
  11.6 0.0 all-reduce.7.cloned.1.call-start
  11.6 175.4 %all-gather.3.cloned.1.call-done = bf16[64,2,12288]{2,1,0:T(2,128)(2,1)} async-done(((bf16[1,2,12288]{2,1,0:T(2,128)(2,1)}), bf16[64,2,12288]{2,1,0:T(2,128)(2,1)}) %all-gather.3.cloned.1.call-update) | async-done | bytes 3145744 | tf_op jit(solution)/shard_map/all_gather | solution.py:21
  187.0 7.3 %reshape.61 = bf16[128,12288]{1,0:T(8,128)(2,1)} reshape(bf16[64,2,12288]{2,1,0:T(2,128)(2,1)} %all-gather.3.cloned.1.call-done) | data formatting | bytes 6291456
  194.4 2.1 fusion.1
  196.5 0.2 copy-done.1
  196.7 3.1 fusion.9
  199.9 2.9 fusion.24
  202.7 5.0 reshape_reshape.6
  207.7 3.9 copy.11
  211.6 0.0 all-reduce.7.cloned.1.call-update
  211.6 0.0 all-reduce.9.cloned.1.call-start
  211.6 1.3 dynamic-slice
  213.6 42.4 %all-reduce.7.cloned.1.call-done = f32[64,2,6144]{2,1,0:T(2,128)} async-done(((f32[64,2,6144]{2,1,0:T(2,128)}), f32[64,2,6144]{2,1,0:T(2,128)}) %all-reduce.7.cloned.1.call-update) | async-done | bytes 3145744
  256.0 2.7 constant_dynamic-slice_fusion.1
  258.7 0.0 all-reduce.9.cloned.1.call-update
  258.7 0.0 all-reduce.11.cloned.1.call-start
  258.8 1.3 dynamic-slice.2
  260.7 4.1 convolution_convert_fusion.1
  264.8 4.1 reshape_reshape.7
  268.9 2.4 convolution_convert_fusion
  271.3 0.7 copy.14
  272.0 1.9 copy.13
  273.9 122.5 %all-reduce.9.cloned.1.call-done = f32[32,2,6144]{2,1,0:T(2,128)} async-done(((f32[32,2,6144]{2,1,0:T(2,128)}), f32[32,2,6144]{2,1,0:T(2,128)}) %all-reduce.9.cloned.1.call-update) | async-done | bytes 1572880
  396.4 1.5 constant_dynamic-slice_fusion
  398.0 0.0 all-reduce.11.cloned.1.call-update
  398.0 0.2 reduce-scatter.2.cloned.1.call-start
  398.2 8.1 %pad_maximum_fusion = bf16[16,196608]{1,0:T(8,128)(2,1)} fusion(bf16[16,98304]{1,0:T(8,128)(2,1)} %bitcast.34, bf16[16,98304]{1,0:T(8,128)(2,1)} %reshape_reshape.7), kind=kLoop, calls=%fused_computation.2 | loop fusion | flops 12582912 | bytes 12582912 | tf_op jit(solution)/shard_map/concatenate | solution.py:52
  406.3 6.4 %reshape.59 = bf16[24576,128]{1,0:T(8,128)(2,1)} reshape(bf16[16,196608]{1,0:T(8,128)(2,1)} %pad_maximum_fusion) | data formatting | bytes 12582912 | tf_op jit(solution)/shard_map/reshape | solution.py:54
  412.7 1.3 dynamic-slice.4
  414.0 45.0 %all-reduce.11.cloned.1.call-done = f32[2,2,6144]{2,1,0:T(2,128)} async-done(((f32[2,2,6144]{2,1,0:T(2,128)}), f32[2,2,6144]{2,1,0:T(2,128)}) %all-reduce.11.cloned.1.call-update) | async-done | bytes 98320
  459.0 1.7 multiply_reduce_fusion
  460.7 13.3 %psum.35 = f32[6144]{0:T(1024)S(1)} all-reduce(f32[6144]{0:T(1024)S(1)} %get-tuple-element.4), channel_id=1, replica_groups=mesh['dp_0'=4,'dp_1'=4,'mp_0'=16,'mp_1'=2,'mp_2'=2] {'dp_0'}, use_global_device_ids=true, to_apply=%region_9.0 | all-reduce | flops 6144 | bytes 49152 | tf_op jit(solution)/shard_map/psum | solution.py:46
  473.9 14.0 %psum.36 = f32[6144]{0:T(1024)S(1)} all-reduce(f32[6144]{0:T(1024)S(1)} %psum.35), channel_id=1, replica_groups=mesh['dp_0'=4,'dp_1'=4,'mp_0'=16,'mp_1'=2,'mp_2'=2] {'dp_1'}, use_global_device_ids=true, to_apply=%region_10.0 | all-reduce | flops 6144 | bytes 49152 | tf_op jit(solution)/shard_map/psum | solution.py:46
  487.9 49.0 %psum.37 = f32[6144]{0:T(1024)S(1)} all-reduce(f32[6144]{0:T(1024)S(1)} %psum.36), channel_id=1, replica_groups=mesh['dp_0'=4,'dp_1'=4,'mp_0'=16,'mp_1'=2,'mp_2'=2] {'mp_0'}, use_global_device_ids=true, to_apply=%region_11.0 | all-reduce | flops 6144 | bytes 49152 | tf_op jit(solution)/shard_map/psum | solution.py:46
  536.9 12.7 %psum.38 = f32[6144]{0:T(1024)S(1)} all-reduce(f32[6144]{0:T(1024)S(1)} %psum.37), channel_id=1, replica_groups=mesh['dp_0'=4,'dp_1'=4,'mp_0'=16,'mp_1'=2,'mp_2'=2] {'mp_1'}, use_global_device_ids=true, to_apply=%region_12.0 | all-reduce | flops 6144 | bytes 49152 | tf_op jit(solution)/shard_map/psum | solution.py:46
  549.6 22.8 %psum.39 = f32[6144]{0:T(1024)S(1)} all-reduce(f32[6144]{0:T(1024)S(1)} %psum.38), channel_id=1, replica_groups=mesh['dp_0'=4,'dp_1'=4,'mp_0'=16,'mp_1'=2,'mp_2'=2] {'mp_2'}, use_global_device_ids=true, to_apply=%region_13.14 | all-reduce | flops 6144 | bytes 49152 | tf_op jit(solution)/shard_map/psum | solution.py:46
  572.4 0.6 broadcast_multiply_fusion
  573.0 2.2 multiply_convert_fusion.4
  575.2 37.3 %reduce-scatter.2.cloned.1.call-done = bf16[1536,128]{1,0:T(8,128)(2,1)} async-done(((bf16[24576,128]{1,0:T(8,128)(2,1)}), bf16[1536,128]{1,0:T(8,128)(2,1)}) %reduce-scatter.2.cloned.1.call-update) | async-done | bytes 393232 | tf_op jit(solution)/shard_map/reduce_scatter | solution.py:55
  612.5 1.1 multiply_convert_fusion
  613.6 0.7 convert_element_type.50
  614.3 0.8 convert_element_type.53
  (9 shorter events, 0.1 us)
Async XLA Ops:
  7.2 187.2 %copy-start = (bf16[6144,256]{1,0:T(8,128)(2,1)S(1)}, bf16[6144,256]{1,0:T(8,128)(2,1)}, u32[]{:S(2)}) copy-start(bf16[6144,256]{1,0:T(8,128)(2,1)} %param.7) | copy-start | bytes 9437188
  7.2 179.9 %all-gather.3.cloned.1.call-start = ((), (), s32[]{:S(2)}) async-start(), calls=%async_computation.2 | async-start | bytes 3194880 | tf_op jit(solution)/shard_map/all_gather | solution.py:21
  11.6 244.4 %all-reduce.7.cloned.1.call-start = ((), (), s32[]{:S(2)}) async-start(), calls=%async_computation.3 | async-start | bytes 6291456
  194.4 2.4 copy-start.1
  211.6 184.8 %all-reduce.9.cloned.1.call-start = ((), (), s32[]{:S(2)}) async-start(), calls=%async_computation.4 | async-start | bytes 3145728
  258.7 200.3 %all-reduce.11.cloned.1.call-start = ((), (), s32[]{:S(2)}) async-start(), calls=%async_computation.5 | async-start | bytes 196608
  398.0 214.5 %reduce-scatter.2.cloned.1.call-start = ((), (), s32[]{:S(2)}) async-start(), calls=%async_computation.1 | async-start | bytes 6684672 | tf_op jit(solution)/shard_map/reduce_scatter | solution.py:55
  412.7 46.3 %copy-start.2 = (f32[6144]{0:T(1024)S(1)}, f32[6144]{0:T(1024)}, u32[]{:S(2)}) copy-start(f32[6144]{0:T(1024)} %param.6) | copy-start | bytes 73732
Sparse Core Ops, SparseCore 0:
  13.0 173.9 all-gather.2
  211.7 44.2 all-reduce.6
  258.8 137.5 all-reduce.8
  400.3 58.6 all-reduce.10
  462.3 150.1 reduce-scatter.1
where the time goes:
time: 623 us; the launch traced here: 622 us
  waiting for transfers between devices  423 us (68%)
  blocking collectives  112 us (18%)
  local copies, waits for them, and re-layouts  39.1 us (6%)
  other arithmetic  17.9 us (3%)
  between operations  15.2 us (2%)
  matrix products  14.6 us (2%)
    unnamed x8, waiting for transfers between devices  210 us
    all_gather x1, waiting for transfers between devices, side_by_side(): lax.all_gather(both, axis, axis=dim, tiled=True)  175 us
    psum x5, blocking collectives, over_axes(): return functools.reduce(lax.psum, axes, shard)  112 us
    reduce_scatter x1, waiting for transfers between devices, sum_packed(): lax.psum_scatter(lines, axis, tiled=True).reshape(-1)  37.3 us
    unnamed x13, local copies, waits for them, and re-layouts  16.3 us
  transfers between devices with their start and end apart: 5, of which 5 were waited for; matrix products, arithmetic and copies ran while one was open for 6% of the time, Pallas kernels for 0%

commit v1 on v0

v1 whole, which is shorter than its diff:
```python
import functools
import math

import jax
import jax.numpy as jnp
from jax import lax
from jax.experimental import pallas as pl
from jax.experimental.pallas import tpu as pltpu
from jax.sharding import Mesh
from jax.sharding import PartitionSpec as P

MP = ("mp_0", "mp_1", "mp_2")
DP = ("dp_0", "dp_1")
DP_MP = ("dp_0", "dp_1", "mp_0", "mp_1", "mp_2")
MESH = pl.DeviceIdType.MESH
GATHER_CUTS = 2
SUM_CUTS = 2
VMEM = pl.BlockSpec(memory_space=pltpu.VMEM)


def place():
    x, y_lo = lax.axis_index("dp_0"), lax.axis_index("dp_1")
    z, y_hi, core = (lax.axis_index(a) for a in MP)
    return x, y_lo, z, y_hi, core


def at_y(y):
    y = lax.rem(y, 8)
    return {"dp_1": lax.rem(y, 4), "mp_1": lax.div(y, 4)}


def remote(src, dst, send, recv, to):
    return pltpu.make_async_remote_copy(
        src_ref=src, dst_ref=dst, send_sem=send, recv_sem=recv, device_id=to, device_id_type=MESH
    )


def await_bytes(ref, sem):
    pltpu.make_async_copy(ref, ref, sem).wait()


def greet(to):
    pl.semaphore_signal(pltpu.get_barrier_semaphore(), inc=1, device_id=to, device_id_type=MESH)


def normalised(tokens):
    values = tokens.astype(jnp.float32)
    centered = values - jnp.mean(values, axis=1, keepdims=True)
    inv_std = lax.rsqrt(jnp.mean(centered * centered, axis=1, keepdims=True) + 1e-06)
    return centered * inv_std, inv_std


def gather_kernel(
    tok, cot, gain, ring, other, cols, mine, stage, tile,
    pair_send, pair_recv, send_r, send_l, recv_l, recv_r, side_send, side_recv, cols_send, cols_recv,
):
    x, y_lo, z, y_hi, core = place()
    slots, _, width = ring.shape
    half = slots // 2
    block = cols.shape[3]
    cuts = GATHER_CUTS
    cut = width // cuts
    y = y_hi * 4 + y_lo
    which = lax.rem(y_hi + core, 2)
    dp = x * 4 + y_lo
    right, left = lax.rem(z + 1, slots), lax.rem(z + slots - 1, slots)
    flip_y, flip_core = 1 - y_hi, 1 - core

    def steps_y(turn):
        return (0, 1, 7, 2 + 4 * which)[turn]

    for to in (
        {"mp_2": flip_core},
        {"mp_1": flip_y},
        {"mp_1": flip_y, "mp_2": flip_core},
        {"mp_0": right},
        {"mp_0": left},
    ):
        greet(to)
    for turn in range(4):
        def hello(dx, _, turn=turn):
            there = at_y(y + 8 - steps_y(turn))
            greet({"dp_0": lax.rem(x + 4 - dx, 4), **there, "mp_2": lax.rem(which + there["mp_1"], 2)})
            return 0
        lax.fori_loop(1 if turn == 0 else 0, 4, hello, 0)

    x_hat, _ = normalised(tok[...])
    mine[0] = (x_hat * gain[...]).astype(jnp.bfloat16)
    mine[1] = cot[...]

    pl.semaphore_wait(pltpu.get_barrier_semaphore(), 20)

    first = remote(mine, stage.at[0], pair_send.at[0], pair_recv.at[0], {"mp_1": flip_y, "mp_2": flip_core})
    across = remote(mine, stage.at[1], pair_send.at[0], pair_recv.at[1], {"mp_1": flip_y})
    beside = remote(mine, stage.at[1], pair_send.at[1], pair_recv.at[1], {"mp_2": flip_core})

    @pl.when(core == 0)
    def _():
        first.start()
        stage[0] = mine[...]

    @pl.when(core == 1)
    def _():
        beside.start()
        across.start()
        first.wait_recv()

    across.wait_recv()
    for kind in range(2):
        @pl.when(which == kind)
        def _(kind=kind):
            for t in range(2):
                for k in range(2):
                    tile[pl.ds(((t + kind) % 2) * 4 + 2 * k, 2), :] = stage[k, t].astype(jnp.float32)
    ring[0] = tile[...].astype(jnp.bfloat16)

    def part(slot, q):
        return ring.at[slot, :, pl.ds(q * cut, cut)]

    def hop_right(s, q):
        return remote(part(s, q), part(s + 1, q), send_r.at[s, q], recv_l.at[s, q], {"mp_0": right})

    def hop_left(s, q):
        here = (slots - s) % slots
        return remote(part(here, q), part(slots - s - 1, q), send_l.at[s, q], recv_r.at[s, q], {"mp_0": left})

    def pass_on(slot):
        remote(ring.at[slot], other.at[slot], side_send, side_recv, {"mp_2": flip_core}).start()

    def spread(lo, n):
        for turn in range(4):
            def to_column(dx, _, turn=turn):
                there = at_y(y + steps_y(turn))
                x_to = lax.rem(x + dx, 4)
                start = pl.multiple_of((x_to * 4 + there["dp_1"]) * block, 128)
                remote(
                    ring.at[pl.ds(lo, n), :, pl.ds(start, block)],
                    cols.at[dp, pl.ds(lo, n)],
                    cols_send,
                    cols_recv,
                    {"dp_0": x_to, **there, "mp_2": lax.rem(which + there["mp_1"], 2)},
                ).start()
                return 0
            lax.fori_loop(1 if turn == 0 else 0, 4, to_column, 0)

    goes_r = lambda s, q: s + 1 < half or q < cuts // 2
    goes_l = lambda s, q: s + 1 < half or q >= cuts // 2
    for s in range(half + 1):
        for q in range(cuts):
            if s > 0 and goes_r(s - 1, q):
                hop_right(s - 1, q).wait_recv()
            if s < half and goes_r(s, q):
                hop_right(s, q).start()
            if s > 0 and goes_l(s - 1, q):
                hop_left(s - 1, q).wait_recv()
            if s < half and goes_l(s, q):
                hop_left(s, q).start()
        pass_on(s)
        if 0 < s < half:
            pass_on(slots - s)
        if s == 2:
            spread(0, 3)
            spread(slots - 2, 2)
        elif s == half:
            spread(s - 1, 3)
        elif s > 2 and s % 2 == 0:
            spread(s - 1, 2)
            spread(slots - s, 2)
    cols[dp] = ring[:, :, pl.ds(pl.multiple_of(dp * block, 128), block)]

    for s in range(half):
        for q in range(cuts):
            if goes_r(s, q):
                hop_right(s, q).wait_send()
            if goes_l(s, q):
                hop_left(s, q).wait_send()

    first.wait_send()

    @pl.when(core == 1)
    def _():
        beside.wait_send()

    await_bytes(other, side_recv)
    await_bytes(ring, side_send)
    most = cols.at[pl.ds(0, cols.shape[0] - 1)]
    await_bytes(most, cols_recv)
    await_bytes(most, cols_send)


def gather_rows(tokens, out_grad, gain, slots, replicas):
    width = tokens.shape[1]
    rows = jax.ShapeDtypeStruct((slots, 8, width), jnp.bfloat16)
    cols = jax.ShapeDtypeStruct((replicas, slots, 8, width // replicas), jnp.bfloat16)
    dma = pltpu.SemaphoreType.DMA
    hops = (slots // 2, GATHER_CUTS)
    return pl.pallas_call(
        gather_kernel,
        name="gather_rows",
        out_shape=(rows, rows, cols),
        in_specs=[VMEM] * 3,
        out_specs=[VMEM] * 3,
        scratch_shapes=[
            pltpu.VMEM((2, 2, width), jnp.bfloat16),
            pltpu.VMEM((2, 2, 2, width), jnp.bfloat16),
            pltpu.VMEM((8, width), jnp.float32),
            dma((2,)), dma((2,)), dma(hops), dma(hops), dma(hops), dma(hops), dma, dma, dma, dma,
        ],
        compiler_params=pltpu.CompilerParams(collective_id=1, has_side_effects=True),
    )(tokens, out_grad, gain)


def exchange_kernel(
    ng, pgh, gp, cols, out_ng, pgh_all, out_gain, other_cols,
    side, go_l, go_r, in_l, in_r, give, take, g1, g2, g3, h1, h2,
    side_send, side_recv, cols_send, cols_recv, send_l, recv_l, send_r, recv_r,
    give_send, take_recv, all_send, all_recv, gain_send, gain_recv,
):
    x, y_lo, z, y_hi, core = place()
    slots, _, width = ng.shape
    half = slots // 2
    part = width // 2
    cuts = SUM_CUTS
    cut = part // cuts
    dp = x * 4 + y_lo
    me = y_hi * 2 + core
    right, left = lax.rem(z + 1, slots), lax.rem(z + slots - 1, slots)
    flip_core = 1 - core

    def dp_peer(k):
        there = lax.rem(dp + k, 16)
        return there, {"dp_0": lax.div(there, 4), "dp_1": lax.rem(there, 4)}

    def quad_peer(k):
        there = lax.rem(me + k, 4)
        return there, {"mp_1": lax.div(there, 2), "mp_2": lax.rem(there, 2)}

    def z_peer(k):
        there = lax.rem(z + k, slots)
        return there, {"mp_0": there}

    for peer, n in ((z_peer, slots), (dp_peer, 16), (quad_peer, 4)):
        lax.fori_loop(1, n, lambda k, _, peer=peer: (greet(peer(k)[1]), 0)[1], 0)
    pl.semaphore_wait(pltpu.get_barrier_semaphore(), slots - 1 + 15 + 3)

    away = pl.multiple_of(flip_core * part, 128)
    home = pl.multiple_of(core * part, 128)
    pieces = ((half - 2, 5), (half - 5, 3), (half + 3, 3), (0, half - 5), (half + 6, slots - half - 6))

    def beside(i):
        lo, n = pieces[i]
        return remote(
            ng.at[pl.ds(lo, n), :, pl.ds(away, part)], side.at[pl.ds(lo, n)], side_send.at[i], side_recv.at[i],
            {"mp_2": flip_core},
        )

    beside(0).start()

    def piece_to(x_from, y_from, to, src=None):
        slot = x_from * 4 + y_from
        here = pgh_all.at[slot] if src is None else src
        return remote(here, pgh_all.at[slot], all_send, all_recv.at[slot], to)

    x_up, x_down = lax.rem(x + 1, 4), lax.rem(x + 3, 4)
    forward = lax.rem(x + 1 + 2 * core, 4)
    behind = lax.rem(x + 3 + 2 * core, 4)
    far = lax.rem(x + 2, 4)

    piece_to(x, y_lo, {"dp_0": x_up}, pgh).start()
    piece_to(x, y_lo, {"dp_0": x_down}, pgh).start()
    for k in range(1, 4):
        piece_to(x, y_lo, {"dp_1": lax.rem(y_lo + k, 4)}, pgh).start()

    def gain_hop(peer, n, src, dst, slot, stage):
        def send(k, _):
            there, to = peer(k)
            remote(src(there), dst.at[slot], gain_send.at[stage], gain_recv.at[stage], to).start()
            return 0
        lax.fori_loop(1, n, send, 0)

    def gain_end(dst, n, stage):
        await_bytes(dst.at[pl.ds(0, n - 1)], gain_recv.at[stage])

    def total(ref, n):
        acc = ref[0]
        for k in range(1, n):
            acc = acc + ref[k]
        return acc

    gain_hop(dp_peer, 16, lambda there: gp.at[there], g1, dp, 0)
    g1[dp] = gp[dp]
    for i in range(1, len(pieces)):
        beside(i).start()
    to_side = remote(cols, other_cols, cols_send, cols_recv, {"mp_2": flip_core})
    to_side.start()
    pgh_all[dp] = pgh[...]

    def own(slot, q):
        here = ng[slot, :, pl.ds(pl.multiple_of(home + q * cut, 128), cut)]
        return here.astype(jnp.float32) + side[slot, :, pl.ds(q * cut, cut)].astype(jnp.float32)

    def hop_l(t, q):
        at = (t, slice(None), pl.ds(q * cut, cut))
        return remote(go_l.at[at], in_l.at[at], send_l.at[t, q], recv_l.at[t, q], {"mp_0": left})

    def hop_r(t, q):
        at = (t, slice(None), pl.ds(q * cut, cut))
        return remote(go_r.at[at], in_r.at[at], send_r.at[t, q], recv_r.at[t, q], {"mp_0": right})

    goes_l = lambda t, q: t > 0 or q < cuts // 2
    goes_r = lambda t, q: t > 0 or q >= cuts // 2
    needed = {0: (0,), 3: (1, 2), 6: (3, 4)}

    for t in range(half):
        for i in needed.get(t, ()):
            beside(i).wait_recv()
        for q in range(cuts):
            cols_q = pl.ds(q * cut, cut)
            if goes_l(t, q):
                value = own(half - t, q)
                if t > 0 and goes_l(t - 1, q):
                    hop_l(t - 1, q).wait_recv()
                    value = value + in_l[t - 1, :, cols_q].astype(jnp.float32)
                go_l[t, :, cols_q] = value.astype(jnp.bfloat16)
                hop_l(t, q).start()
            if goes_r(t, q):
                value = own(half + t, q)
                if t > 0 and goes_r(t - 1, q):
                    hop_r(t - 1, q).wait_recv()
                    value = value + in_r[t - 1, :, cols_q].astype(jnp.float32)
                go_r[t, :, cols_q] = value.astype(jnp.bfloat16)
                hop_r(t, q).start()
        if t == 1:
            piece_to(behind, y_lo, {"dp_0": forward}).wait_recv()
            piece_to(behind, y_lo, {"dp_0": forward}).start()
            gain_end(g1, 16, 0)
            h1[...] = total(g1, 16)
            g2[me] = h1[...]
            gain_hop(quad_peer, 4, lambda there: h1, g2, me, 1)
        if t in (2, 3, 4):
            y_from = lax.rem(y_lo + t - 1, 4)
            piece_to(x, y_from, {"dp_0": x_up}).wait_recv()
            piece_to(x, y_from, {"dp_0": x_up}).start()
            piece_to(x, y_from, {"dp_0": x_down}).start()
        if t == 3:
            gain_end(g2, 4, 1)
            h2[...] = total(g2, 4)
            g3[z] = h2[...]
            gain_hop(z_peer, slots, lambda there: h2, g3, z, 2)
        if t in (4, 5, 6):
            y_from = lax.rem(y_lo + t - 3, 4)
            piece_to(behind, y_from, {"dp_0": forward}).wait_recv()
            piece_to(behind, y_from, {"dp_0": forward}).start()

    gain_end(g3, slots, 2)
    h1_out = total(g3, slots)
    out_gain[dp] = h1_out
    gain_hop(dp_peer, 16, lambda there: out_gain.at[dp], out_gain, dp, 3)

    for q in range(cuts):
        hop_l(half - 1, q).wait_recv()
        hop_r(half - 1, q).wait_recv()
        cols_q = pl.ds(q * cut, cut)
        value = own(0, q) + in_l[half - 1, :, cols_q].astype(jnp.float32) + in_r[half - 1, :, cols_q].astype(jnp.float32)
        for k in range(4):
            give[k, :, cols_q] = value[2 * k : 2 * k + 2]

    def hand(k, _):
        there, to = quad_peer(k)
        remote(give.at[there], take.at[me], give_send, take_recv, to).start()
        return 0
    lax.fori_loop(1, 4, hand, 0)
    take[me] = give[me]

    for t in range(half):
        for q in range(cuts):
            if goes_l(t, q):
                hop_l(t, q).wait_send()
            if goes_r(t, q):
                hop_r(t, q).wait_send()
    for i in range(len(pieces)):
        beside(i).wait_send()
    for k in range(4):
        y_from = lax.rem(y_lo + k, 4)
        piece_to(forward, y_from, {"dp_0": forward}).wait_recv()
        piece_to(far, y_from, {"dp_0": forward}).wait_recv()
    await_bytes(pgh_all.at[pl.ds(0, 15)], all_send)
    to_side.wait_recv()
    to_side.wait_send()

    await_bytes(take.at[pl.ds(0, 3)], take_recv)
    await_bytes(give.at[pl.ds(0, 3)], give_send)
    out_ng[:, pl.ds(0, part)] = take[0] + take[2]
    out_ng[:, pl.ds(part, part)] = take[1] + take[3]
    gain_end(out_gain, 16, 3)
    for dst, n, stage in ((g1, 16, 0), (g2, 4, 1), (g3, slots, 2), (out_gain, 16, 3)):
        await_bytes(dst.at[pl.ds(0, n - 1)], gain_send.at[stage])


def exchange(ng, pgh, gp, cols):
    slots, _, width = ng.shape
    part, half = width // 2, slots // 2
    replicas, _, block = gp.shape
    dma = pltpu.SemaphoreType.DMA
    bf16, f32 = jnp.bfloat16, jnp.float32
    hops = (half, SUM_CUTS)
    line = pltpu.VMEM((half, 8, part), bf16)
    return pl.pallas_call(
        exchange_kernel,
        name="exchange",
        out_shape=(
            jax.ShapeDtypeStruct((2, width), f32),
            jax.ShapeDtypeStruct((replicas, *pgh.shape), bf16),
            jax.ShapeDtypeStruct(gp.shape, f32),
            jax.ShapeDtypeStruct(cols.shape, bf16),
        ),
        in_specs=[VMEM] * 4,
        out_specs=[VMEM] * 4,
        scratch_shapes=[
            pltpu.VMEM((slots, 8, part), bf16), line, line, line, line,
            pltpu.VMEM((4, 2, part), f32), pltpu.VMEM((4, 2, part), f32),
            pltpu.VMEM((16, 1, block), f32), pltpu.VMEM((4, 1, block), f32), pltpu.VMEM((slots, 1, block), f32),
            pltpu.VMEM((1, block), f32), pltpu.VMEM((1, block), f32),
            dma((5,)), dma((5,)), dma, dma, dma(hops), dma(hops), dma(hops), dma(hops),
            dma, dma, dma, dma((16,)), dma((4,)), dma((4,)),
        ],
        compiler_params=pltpu.CompilerParams(collective_id=2, has_side_effects=True),
    )(ng, pgh, gp, cols)


def gelu_value(preact):
    return 0.5 * preact * (1.0 + lax.erf(preact * 0.7071067811865476))


def gelu_slope(preact):
    return (
        0.5 * (1.0 + lax.erf(preact * 0.7071067811865476))
        + preact * jnp.exp(-0.5 * preact * preact) * 0.3989422804014327
    )


def contract_rows(left, right):
    return lax.dot_general(
        left, right, (((0,), (0,)), ((), ())), preferred_element_type=jnp.float32
    )


def contract_cols(left, right):
    return lax.dot_general(
        left, right, (((1,), (1,)), ((), ())), preferred_element_type=jnp.float32
    )


def swap_halves(rows):
    return jnp.roll(rows.reshape(-1, 8, rows.shape[1]), 4, axis=1).reshape(rows.shape)


def per_device(tokens, norm_gain, up_weight, down_weight, out_grad):
    slots, replicas = lax.axis_size("mp_0"), lax.axis_size(DP)
    width = tokens.shape[1]
    group = slots * 8
    ring, other, cols = gather_rows(tokens, out_grad, norm_gain[None], slots, replicas)

    own_first = lax.rem(lax.axis_index("mp_1") + lax.axis_index("mp_2"), 2) == 0
    pick = (lax.broadcasted_iota(jnp.int32, (1, 8, 1), 1) < 4) == own_first
    normed = jnp.where(pick, ring, other).reshape(group, width)
    cotan = jnp.where(pick, other, ring).reshape(group, width)

    preact = jnp.dot(normed, up_weight, preferred_element_type=jnp.float32)
    hid_grad = swap_halves(contract_cols(cotan, down_weight))
    hidden = swap_halves(gelu_value(preact)).astype(jnp.bfloat16)
    pre_grad = (hid_grad * gelu_slope(preact)).astype(jnp.bfloat16)
    partial = contract_cols(pre_grad, up_weight)
    gain_part = jnp.sum(partial * normed.astype(jnp.float32), axis=0)

    norm_grad, both_all, gain_sum, other_cols = exchange(
        partial.astype(jnp.bfloat16).reshape(slots, 8, width),
        jnp.stack([pre_grad, hidden]),
        gain_part.reshape(replicas, 1, width // replicas),
        cols,
    )

    factor = 1.0 / math.sqrt(group * replicas)
    gain_grad = gain_sum.reshape(width) / norm_gain * factor
    x_hat, inv_std = normalised(tokens)
    scaled = norm_gain * norm_grad
    input_grad = (
        scaled
        - jnp.mean(scaled, axis=1, keepdims=True)
        - x_hat * jnp.mean(scaled * x_hat, axis=1, keepdims=True)
    ) * inv_std

    pick = pick[None]
    block = width // replicas
    normed_cols = jnp.where(pick, cols, other_cols).reshape(-1, block)
    cotan_cols = jnp.where(pick, other_cols, cols).reshape(-1, block)
    pre_all = both_all[:, 0].reshape(-1, up_weight.shape[1])
    hid_all = both_all[:, 1].reshape(-1, up_weight.shape[1])
    up_grad = (contract_rows(normed_cols, pre_all) * factor).astype(jnp.bfloat16)
    down_grad = (contract_rows(hid_all, cotan_cols) * factor).astype(jnp.bfloat16)
    return (input_grad.astype(jnp.bfloat16), up_grad, down_grad, gain_grad)


def solution(mesh):
    torus = Mesh(mesh.devices.reshape(4, 4, 16, 2, 2), ("dp_0", "dp_1", "mp_0", "mp_1", "mp_2"))
    return jax.shard_map(
        per_device,
        mesh=torus,
        in_specs=(P(DP_MP, None), P(), P(None, MP), P(MP, None), P(DP_MP, None)),
        out_specs=(P(DP_MP, None), P(DP, MP), P(MP, DP), P()),
        check_vma=False,
    )
```

time: 623 us -> 131 us (0.21)
  waiting for transfers between devices: 423 us -> 0 us
  Pallas kernels: 0 us -> 112 us
  blocking collectives: 112 us -> 0 us
  local copies, waits for them, and re-layouts: 39.1 us -> 0.37 us
  between operations: 15.2 us -> 0.77 us
  other arithmetic: 17.9 us -> 6.72 us
    unnamed x8 -> x0, waiting for transfers between devices: 210 us -> none
    all_gather x1 -> x0, waiting for transfers between devices: 175 us -> none  [side_by_side(): lax.all_gather(both, axis, axis=dim, tiled=True)]
    pallas_call x0 -> x2, Pallas kernels: none -> 112 us  [the longest x1 60.6 us: gather_rows(): pl.pallas_call(gather_kernel, name='gather_rows', out_shape=(rows, rows,...]
    psum x5 -> x0, blocking collectives: 112 us -> none  [over_axes(): return functools.reduce(lax.psum, axes, shard)]
    reduce_scatter x1 -> x0, waiting for transfers between devices: 37.3 us -> none  [sum_packed(): lax.psum_scatter(lines, axis, tiled=True).reshape(-1)]
    unnamed x13 -> x14, local copies, waits for them, and re-layouts: 16.3 us -> 0.19 us
    another operation x2 -> x0, local copies, waits for them, and re-layouts: 9.05 us -> none  [the longest x1 4.98 us: sum_in_order(): blocks = blocks.reshape(*lengths, *blocks.shape[1:])]
    reshape x2 -> x0, local copies, waits for them, and re-layouts: 8.31 us -> none  [the longest x1 6.37 us: sum_packed(): jnp.pad(lines, ((0, 0), (0, width * 128 - lines.shape[1]))).reshape(-1, 128)]
  transfers between devices with their start and end apart: 5 -> 0, of which waited for: 5 -> 0; matrix products, arithmetic and copies ran while one was open for 6% -> 0% of each run, Pallas kernels for 0% -> 0%
where the time goes in v1:
time: 131 us; the launch traced here: 130 us
  Pallas kernels  112 us (85%)
  matrix products  10.6 us (8%)
  other arithmetic  6.72 us (5%)
    pallas_call x1, Pallas kernels, gather_rows(): pl.pallas_call(gather_kernel, name='gather_rows', out_shape=(rows, rows,...  60.6 us
    pallas_call x1, Pallas kernels, exchange(): pl.pallas_call(exchange_kernel, name='exchange', out_shape=(jax.ShapeDtyp...  51.4 us
    dot_general x2, matrix products, contract_cols(): lax.dot_general(left, right, (((1,), (1,)), ((), ())), preferred_element_...  7.17 us
    dot_general x2, matrix products, contract_rows(): lax.dot_general(left, right, (((0,), (0,)), ((), ())), preferred_element_...  2.74 us

profile of v1, /device:TPU:1, one launch (start us, length us, event | category | flops | bytes accessed | tf_op | source)
XLA Modules:
  0.0 130.5 jit_solution(11827161563736727566)
XLA Ops:
  0.6 0.0 copy-start
  0.6 60.6 %gather_rows.1 = (bf16[16,8,6144]{2,1,0:T(8,128)(2,1)}, bf16[16,8,6144]{2,1,0:T(8,128)(2,1)}, bf16[16,16,8,384]{3,2,1,0:T(8,128)(2,1)}) custom-call(bf16[2,6144]{1,0:T(2,128)(2,1)} %tok.1, bf16[2,6144]{1,0:T(2,128)(2,1)} %cot.1, f32[1,6144]{1,0:T(1,128)} %bitcast.38), custom_call_target="tpu_custom_call" | custom-call | tf_op jit(solution)/shard_map/gather_rows/pallas_call | solution.py:197
  61.3 0.0 copy-start.1
  61.3 0.0 copy-start.2
  61.3 4.2 %fusion = f32[16,8,256]{2,1,0:T(8,128)S(1)} fusion(bf16[256,6144]{1,0:T(8,128)(2,1)} %param.8, bf16[16,8,6144]{2,1,0:T(8,128)(2,1)} %get-tuple-element.11, bf16[16,8,6144]{2,1,0:T(8,128)(2,1)} %get-tuple-element.12, pred[8]{0:T(512)(128)(4,1)S(1)} %compare_compare_fusion), kind=kOutput, calls=%fused_computation | convolution fusion | flops 403439616 | bytes 6422536 | tf_op jit(solution)/shard_map/dot_general | solution.py:449
  65.5 0.0 copy-done
  65.5 0.0 copy-done.1
  65.5 0.0 copy-done.2
  65.5 0.7 fusion.14
  66.2 3.0 %multiply_reduce_fusion = (f32[6144]{0:T(1024)}, bf16[16,8,6144]{2,1,0:T(8,128)(2,1)}) fusion(bf16[16,8,6144]{2,1,0:T(8,128)(2,1)S(1)} %copy-done.1, bf16[16,8,6144]{2,1,0:T(8,128)(2,1)S(1)} %copy-done.2, pred[8]{0:T(512)(128)(4,1)S(1)} %compare_compare_fusion, bf16[128,256]{1,0:T(8,128)(2,1)S(1)} %get-tuple-element.27, bf16[6144,256]{1,0:T(8,128)(2,1)S(1)} %copy-done), kind=kOutput, calls=%fused_computation.2 | convolution fusion | flops 406579200 | bytes 7954440 | tf_op jit(solution)/shard_map/dot_general | solution.py:449
  69.3 0.7 pad_maximum_fusion.pgh
  70.0 0.0 copy-start.4
  70.0 0.0 copy-start.5
  70.0 51.4 %exchange.1 = (f32[2,6144]{1,0:T(2,128)}, bf16[16,2,128,256]{3,2,1,0:T(8,128)(2,1)}, f32[16,1,384]{2,1,0:T(1,128)}, bf16[16,16,8,384]{3,2,1,0:T(8,128)(2,1)}) custom-call(bf16[16,8,6144]{2,1,0:T(8,128)(2,1)} %get-tuple-element.23.ng, bf16[2,128,256]{2,1,0:T(8,128)(2,1)} %pad_maximum_fusion.pgh, f32[16,1,384]{2,1,0:T(1,128)} %bitcast.40, ...), custom_call_target="tpu_custom_call" | custom-call | tf_op jit(solution)/shard_map/exchange/pallas_call | solution.py:408
  121.4 0.0 copy-done.4
  121.4 0.2 convert_reduce_fusion
  121.6 0.2 fusion.17
  121.8 0.0 copy-done.5
  121.9 1.1 multiply_reduce_fusion.2
  122.9 1.5 %multiply_convert_fusion.1 = bf16[2,6144]{1,0:T(2,128)(2,1)} fusion(bf16[2,6144]{1,0:T(2,128)(2,1)S(1)} %copy-done.4, f32[2,6144]{1,0:T(2,128)} %get-tuple-element.14, f32[2]{0:T(128)S(1)} %get-tuple-element.32, f32[2]{0:T(128)S(1)} %add_rsqrt_fusion, f32[2]{0:T(128)S(1)} %broadcast_multiply_fusion.1, f32[2]{0:T(128)S(1)} %get-tuple-element.33, ...), kind=kLoop, calls=%fused_computation.33 | loop fusion | flops 110592 | bytes 122912 | tf_op jit(solution)/shard_map/convert_element_type | solution.py:501
  124.5 0.0 copy-start.3
  124.5 2.4 %broadcast_select_fusion = (bf16[16,16,8,384]{3,2,1,0:T(8,128)(2,1)S(1)}, bf16[16,16,8,384]{3,2,1,0:T(8,128)(2,1)S(1)}) fusion(bf16[16,16,8,384]{3,2,1,0:T(8,128)(2,1)} %get-tuple-element.15, bf16[16,16,8,384]{3,2,1,0:T(8,128)(2,1)} %get-tuple-element.13.cols, pred[8]{0:T(512)(128)(4,1)S(1)} %compare_compare_fusion), kind=kLoop, calls=%fused_computation.7 | loop fusion | flops 1572864 | bytes 6291464 | tf_op jit(solution)/shard_map/jit(_where)/select_n | solution.py:496
  126.8 0.2 copy-done.3
  127.0 0.1 fusion.18
  127.1 1.3 %fusion.6 = bf16[384,256]{1,0:T(8,128)(2,1)} fusion(bf16[2048,384]{1,0:T(8,128)(2,1)S(1)} %bitcast.35, bf16[2048,256]{1,0:T(8,128)(2,1)S(1)} %bitcast.37), kind=kOutput, calls=%fused_computation.13 | convolution fusion | flops 402849792 | bytes 2818048 | tf_op jit(solution)/shard_map/dot_general | solution.py:443
  128.5 0.0 copy-start.6
  128.5 1.4 %fusion.7 = bf16[256,384]{1,0:T(8,128)(2,1)} fusion(bf16[2048,256]{1,0:T(8,128)(2,1)S(1)} %bitcast.36, bf16[2048,384]{1,0:T(8,128)(2,1)S(1)} %bitcast.34), kind=kOutput, calls=%fused_computation.14 | convolution fusion | flops 402849792 | bytes 2818048 | tf_op jit(solution)/shard_map/dot_general | solution.py:443
  129.9 0.0 copy-done.6
  129.9 0.6 divide_multiply_fusion
  (7 shorter events, 0.1 us)
Async XLA Ops:
  0.6 64.9 %copy-start = (bf16[6144,256]{1,0:T(8,128)(2,1)S(1)}, bf16[6144,256]{1,0:T(8,128)(2,1)}, u32[]{:S(2)}) copy-start(bf16[6144,256]{1,0:T(8,128)(2,1)} %param.7) | copy-start | bytes 9437188
  61.3 4.2 %copy-start.1 = (bf16[16,8,6144]{2,1,0:T(8,128)(2,1)S(1)}, bf16[16,8,6144]{2,1,0:T(8,128)(2,1)}, u32[]{:S(2)}) copy-start(bf16[16,8,6144]{2,1,0:T(8,128)(2,1)} %get-tuple-element.12) | copy-start | bytes 4718596
  61.3 4.2 %copy-start.2 = (bf16[16,8,6144]{2,1,0:T(8,128)(2,1)S(1)}, bf16[16,8,6144]{2,1,0:T(8,128)(2,1)}, u32[]{:S(2)}) copy-start(bf16[16,8,6144]{2,1,0:T(8,128)(2,1)} %get-tuple-element.11) | copy-start | bytes 4718596
  70.0 51.4 %copy-start.4 = (bf16[2,6144]{1,0:T(2,128)(2,1)S(1)}, bf16[2,6144]{1,0:T(2,128)(2,1)}, u32[]{:S(2)}) copy-start(bf16[2,6144]{1,0:T(2,128)(2,1)} %tok.1) | copy-start | bytes 73732
  70.0 51.9 %copy-start.5 = (f32[6144]{0:T(1024)S(1)}, f32[6144]{0:T(1024)}, u32[]{:S(2)}) copy-start(f32[6144]{0:T(1024)} %param.6) | copy-start | bytes 73732
  124.5 2.5 %copy-start.3 = (bf16[16,2,128,256]{3,2,1,0:T(8,128)(2,1)S(1)}, bf16[16,2,128,256]{3,2,1,0:T(8,128)(2,1)}, u32[]{:S(2)}) copy-start(bf16[16,2,128,256]{3,2,1,0:T(8,128)(2,1)} %get-tuple-element.16) | copy-start | bytes 6291460
  128.5 1.4 %copy-start.6 = (f32[16,1,384]{2,1,0:T(1,128)S(1)}, f32[16,1,384]{2,1,0:T(1,128)}, u32[]{:S(2)}) copy-start(f32[16,1,384]{2,1,0:T(1,128)} %get-tuple-element.17) | copy-start | bytes 73732
